TPU v7x, 32 devices: a whole 2x2x4 slice. The times are simulated.
32 devices in a mesh: dp: 8 (over z, x), section: 4 (over y, core).
Axes of the slice: x: 2, y: 2, z: 4, core: 2. Of those that a mesh axis runs over, the one named last changes fastest.
Arguments:
- hidden_in: bfloat16 [4, 4, 8, 96, 2048], P('section', None, 'dp'), may hold values from -170 to 170
- queries: bfloat16 [4, 4, 8, 96, 2048], P('section', None, 'dp'), may hold values from -96 to 96
- keys: bfloat16 [4, 4, 8, 96, 2048], P('section', None, 'dp'), may hold values from -6 to 6
- values: bfloat16 [4, 4, 8, 96, 2048], P('section', None, 'dp'), may hold values from -6 to 6
- cotangent: bfloat16 [4, 8, 96, 2048], P(None, 'dp'), may hold values from -6 to 6
- norm_gain: float32 [4, 2048], P('section'), may hold values from 0.1 to 1.9
- w_query: bfloat16 [4, 2048, 2048], P('section', 'dp'), may hold values from -0.125 to 0.125
- w_key: bfloat16 [4, 2048, 2048], P('section', 'dp'), may hold values from -0.125 to 0.125
- w_value: bfloat16 [4, 2048, 2048], P('section', 'dp'), may hold values from -0.125 to 0.125
- down_q: bfloat16 [4, 16, 2048], P('section'), may hold values from -0.125 to 0.125
- up_q: bfloat16 [4, 16, 2048], P('section'), may hold values from -0.75 to 0.75
- down_v: bfloat16 [4, 16, 2048], P('section'), may hold values from -0.125 to 0.125
- up_v: bfloat16 [4, 16, 2048], P('section'), may hold values from -0.75 to 0.75
Outputs:
- input_grad: bfloat16 [4, 4, 8, 96, 2048], P('section', None, 'dp')
- grad_down_q: float32 [4, 16, 2048], P('section')
- grad_up_q: float32 [4, 16, 2048], P('section')
- grad_down_v: float32 [4, 16, 2048], P('section')
- grad_up_v: float32 [4, 16, 2048], P('section')
All inputs are finite; a program needn't handle non-finite values.
Results may differ from a plain program's by a relative error of at most 0.025.
Values may be sent and summed in bfloat16 or wider, within the bound.
A program may use at most 128 MiB of HBM per device.

v0:
```python
import functools

import jax
import jax.numpy as jnp
from jax import lax
from jax.experimental import pallas as pl
from jax.experimental.pallas import tpu as pltpu
from jax.sharding import PartitionSpec as P

HEAD_DIM = 128
adapter_scale = 2.0
norm_eps = 1e-05
NN = (((1,), (0,)), ((), ()))
NT = (((1,), (1,)), ((), ()))
TN = (((0,), (0,)), ((), ()))
F32 = jnp.float32
BF16 = jnp.bfloat16
MESH = pl.DeviceIdType.MESH
PAIR = 2


def dot(a, b, dims):
    return lax.dot_general(a, b, dims, preferred_element_type=F32)


def drain(ref, sem):
    pltpu.make_async_copy(ref, ref, sem).wait()


def remote(src, dst, send, recv, device):
    return pltpu.make_async_remote_copy(
        src_ref=src, dst_ref=dst, send_sem=send, recv_sem=recv, device_id=device, device_id_type=MESH
    )


def flip(value, k, size):
    if size & (size - 1):
        return lax.rem(value + k, size)
    out, bit = 0, 1
    while bit < size:
        out = out + bit * lax.rem(lax.div(value, bit) + (k // bit) % 2, 2)
        bit *= 2
    return out


def kernel(
    n_dp, layers, micro, seq, features, rank, rows_w, total_scale,
    hid, que, key, val, cot, gain, wq, wk, wv, dq, uq, dv, uv,
    out_ig, out_g,
    wbuf, act, hown, og, ab, nrm, ad, gn, st, st_own, lows, lowr, lowt,
    cs, crecv, ctmp, cown, xs, xrecv, sc, rs_own, rsr, crow, gr, gf,
    w_s, w_r, q_s, q_r, h_s, h_r, ad_s, ad_r, gn_s, gn_r, cot_s, cot_r, hown_sem, st_s, st_r,
    z_s, z_r, rel_s, lo_s, lo_r, d_s, d_r, x_s, x_r, rs_s, rs_r, o_s, o_r, g_s, g_r, f_s, f_r,
):
    sections = layers
    planes = n_dp // PAIR
    cols = PAIR * sections
    chips = cols // 2
    hw = features // cols
    heads = hw // HEAD_DIM
    seqs = PAIR * micro
    rows = seqs * seq
    block = PAIR * rows_w
    dp, s = lax.axis_index("dp"), lax.axis_index("section")
    a, x = lax.div(dp, PAIR), lax.rem(dp, PAIR)
    f = x * sections + s
    c = lax.rem(f, 2)
    chip = lax.div(f, 2)

    def device(j):
        return (PAIR * a + lax.div(j, sections), lax.rem(j, sections))

    others = [flip(f, k, cols) for k in range(1, cols)]

    def col_of(j):
        return pl.ds(pl.multiple_of(j * hw, hw), hw)

    barrier = pltpu.get_barrier_semaphore()
    for j in others:
        pl.semaphore_signal(barrier, inc=1, device_id=device(j), device_id_type=MESH)
    for k in range(1, planes):
        pl.semaphore_signal(
            barrier, inc=1, device_id=(PAIR * lax.rem(a + k, planes) + x, s), device_id_type=MESH
        )
    pl.semaphore_wait(barrier, cols - 1 + planes - 1)

    own_hidden = pltpu.make_async_copy(hid.at[0, :, 0], hown, hown_sem)
    own_hidden.start()
    for k in range(sections):
        s2 = s if k == 0 else flip(s, k, sections)
        cut = col_of(x * sections + s2)
        for i, ref in enumerate((dq, dv, uq, uv)):
            src, dst = ref.at[0, :, cut], ad.at[s, pl.ds(i * rank, rank), :]
            if k == 0:
                pltpu.make_async_copy(src, dst, ad_r.at[s]).start()
            else:
                remote(src, dst, ad_s.at[k], ad_r.at[s], (dp, s2)).start()
        src, dst = gain.at[:, cut], gn.at[s]
        if k == 0:
            pltpu.make_async_copy(src, dst, gn_r.at[s]).start()
        else:
            remote(src, dst, gn_s.at[k], gn_r.at[s], (dp, s2)).start()
    mirror = (PAIR * a + 1 - x, s)
    remote(cot.at[:, 0, :, col_of((1 - x) * sections + s)], og.at[x], cot_s.at[0], cot_r.at[0], mirror).start()
    pltpu.make_async_copy(cot.at[:, 0, :, col_of(f)], og.at[x], cot_r.at[1]).start()

    def send_big():
        def weights(j):
            for i, ref in enumerate((wq, wk, wv)):
                yield ref.at[0, :, col_of(j)], wbuf.at[s, a, pl.ds(x * rows_w, rows_w), pl.ds(i * hw, hw)]

        def saved(j):
            for i, ref in enumerate((que, key, val)):
                yield ref.at[0, :, 0, :, col_of(j)], act.at[s, x, i]

        def inputs(j):
            yield hid.at[0, :, 0, :, col_of(j)], act.at[s, x, 3]

        for group, send, recv in ((weights, w_s, w_r), (saved, q_s, q_r), (inputs, h_s, h_r)):
            for k, j in enumerate(others):
                for src, dst in group(j):
                    remote(src, dst, send.at[k], recv.at[f], device(j)).start()
            for src, dst in group(f):
                pltpu.make_async_copy(src, dst, recv.at[f]).start()

    early = lax.rem(layers - 1 - s, 2) == 0
    pl.when(early)(send_big)

    eye = lax.broadcasted_iota(jnp.int32, (seq, 128), 0) == lax.broadcasted_iota(jnp.int32, (seq, 128), 1)

    def to_row(column):
        return jnp.sum(jnp.where(eye, column, 0.0), axis=0, keepdims=True)

    def to_column(row):
        return jnp.sum(jnp.where(eye, row, 0.0), axis=1, keepdims=True)

    own_hidden.wait()

    def inverse_of(m, carry):
        floated = hown[m].astype(F32)
        inverse = lax.rsqrt(jnp.mean(floated * floated, axis=-1, keepdims=True) + norm_eps)
        st_own[pl.ds(m, 1), :] = to_row(inverse)
        return carry

    lax.fori_loop(0, micro, inverse_of, 0)
    st[f] = st_own[...]
    for k, j in enumerate(others):
        remote(st_own, st.at[f], st_s.at[k], st_r.at[f], device(j)).start()

    def z_own(l):
        for xx in range(PAIR):
            drain(wbuf.at[l, a, pl.ds(xx * rows_w, rows_w), :], w_r.at[xx * sections + l])
        for i, d in enumerate((2, -2, 1, -1)):
            if abs(d) >= planes:
                continue

            @pl.when((a + d >= 0) & (a + d < planes))
            def _():
                remote(
                    wbuf.at[l, a], wbuf.at[l, a], z_s.at[l, i], z_r.at[l, a], (PAIR * (a + d) + x, s)
                ).start()

    def passed_on(l, b, todo):
        for direction in (1, -1):

            @pl.when(((a - b) * direction >= 2) & (a + direction >= 0) & (a + direction < planes))
            def _():
                todo(
                    remote(
                        wbuf.at[l, b], wbuf.at[l, b], rel_s.at[l, b], z_r.at[l, b],
                        (PAIR * (a + direction) + x, s),
                    )
                )

    def take(l, b):
        drain(wbuf.at[l, b], z_r.at[l, b])
        passed_on(l, b, lambda copy: copy.start())

    scale = HEAD_DIM ** (-0.5)
    causal = lax.broadcasted_iota(jnp.int32, (seq, seq), 1) <= lax.broadcasted_iota(jnp.int32, (seq, seq), 0)
    z_own(layers - 1)

    def finish_grads(l):
        for k in range(1, planes):
            b = lax.rem(a + k, planes)
            drain(gr.at[l, b], g_r.at[l, b])
        total = gr[l, 0].astype(F32)
        for b in range(1, planes):
            total = total + gr[l, b].astype(F32)
        gf[l] = total * total_scale
        for xx in range(PAIR):
            mine = (x == xx) & (s == l)

            @pl.when(mine)
            def _():
                pltpu.make_async_copy(gf.at[l], out_g.at[:, col_of(f)], f_s.at[l, xx]).start()

            @pl.when(jnp.logical_not(mine))
            def _():
                remote(
                    gf.at[l], out_g.at[:, col_of(f)], f_s.at[l, xx], f_r.at[f], (PAIR * a + xx, l)
                ).start()

    def layer(i, carry):
        l = layers - 1 - i
        for xx in range(PAIR):
            drain(act.at[l, xx, pl.ds(0, 3)], q_r.at[xx * sections + l])

        @pl.when(i == 0)
        def _():
            pl.when(jnp.logical_not(early))(send_big)
            drain(og.at[0], cot_r.at[0])
            drain(og.at[0], cot_r.at[1])

        def attention(n, carry):
            xx, m = lax.div(n, micro), lax.rem(n, micro)
            for h in range(heads):
                at = pl.ds(h * HEAD_DIM, HEAD_DIM)
                q, k, v = (act[l, xx, t, m, :, at] for t in range(3))
                g = og[xx, m, :, at]
                scores = jnp.where(causal, dot(q, k, NT) * scale, -1e30)
                grown = jnp.exp(scores - jnp.max(scores, axis=-1, keepdims=True))
                attend = grown / jnp.sum(grown, axis=-1, keepdims=True)
                attend_grad = dot(g, v, NT)
                value_grad = dot(attend.astype(BF16), g, TN)
                row_total = jnp.sum(attend * attend_grad, axis=-1, keepdims=True)
                score_grad = (attend * (attend_grad - row_total) * scale).astype(BF16)
                ab[n, :, at] = dot(score_grad, k, NN).astype(BF16)
                ab[n, :, pl.ds(hw + h * HEAD_DIM, HEAD_DIM)] = dot(score_grad, q, TN).astype(BF16)
                ab[n, :, pl.ds(2 * hw + h * HEAD_DIM, HEAD_DIM)] = value_grad.astype(BF16)
            return carry

        lax.fori_loop(0, seqs, attention, 0)

        for xx in range(PAIR):
            j = xx * sections + l
            drain(act.at[l, xx, 3], h_r.at[j])

            @pl.when(j != f)
            def _():
                drain(st.at[j], st_r.at[j])

        drain(ad.at[l], ad_r.at[l])
        drain(gn.at[l], gn_r.at[l])
        gains = gn[l]

        def normalise(n, carry):
            xx, m = lax.div(n, micro), lax.rem(n, micro)
            inverse = to_column(st[xx * sections + l, pl.ds(m, 1), :])
            nrm[n] = (act[l, xx, 3, m].astype(F32) * inverse * gains).astype(BF16)
            return carry

        lax.fori_loop(0, seqs, normalise, 0)

        def flat(value):
            return value.reshape(rows, value.shape[-1])

        normed = flat(nrm[...])
        down = ad[l, : 2 * rank]
        lows[:rank] = (adapter_scale * dot(ad[l, 2 * rank : 3 * rank], flat(ab[:, :, :hw]), NT)).astype(BF16)
        lows[rank : 2 * rank] = (
            adapter_scale * dot(ad[l, 3 * rank :], flat(ab[:, :, 2 * hw :]), NT)
        ).astype(BF16)
        lows[2 * rank :] = dot(down, normed, NT).astype(BF16)
        for k, j in enumerate(others):
            remote(lows, lowr.at[f], lo_s.at[k], lo_r.at[f], device(j)).start()

        @pl.when(i > 0)
        def _():
            finish_grads(l + 1)

        def next_own():
            @pl.when(l > 0)
            def _():
                z_own(l - 1)

        def half(p, cc):
            start = (2 * p + cc) * hw
            w = wbuf[l, lax.div(start, block), pl.ds(pl.multiple_of(lax.rem(start, block), hw), hw), :]
            return dot(flat(ab[...]), w, NT).reshape(seqs, seq, hw)

        partner = flip(f, 1, cols)

        def pair(p):
            cs[p] = half(p, 1 - c).astype(BF16)
            to_partner = remote(cs.at[p], crecv.at[p], d_s.at[p], d_r.at[p], device(partner))
            to_partner.start()
            ctmp[...] = half(p, c)
            to_partner.wait_recv()

            @pl.when(p == chip)
            def _():
                cown[...] = ctmp[...] + crecv[p].astype(F32)

            @pl.when(p != chip)
            def _():
                xs[p] = (ctmp[...] + crecv[p].astype(F32)).astype(BF16)
                remote(xs.at[p], xrecv.at[chip], x_s.at[p], x_r.at[chip], device(2 * p + c)).start()

        if planes == 4 and chips == 4:
            upper = lax.div(a, 2)
            near = a + upper * (3 - 2 * a)
            for k in range(4):
                lower = lax.rem(near + k, 2) if k < 2 else k
                p = lower + upper * (3 - 2 * lower)
                relays = (a == 1) | (a == 2)
                if k == 3:
                    pl.when(jnp.logical_not(relays))(next_own)
                if k > 0:
                    take(l, p)
                if k == 3:
                    pl.when(relays)(next_own)
                pair(p)
        else:
            for d in range(1, planes):
                for b in (a - d, a + d):

                    @pl.when((b >= 0) & (b < planes))
                    def _():
                        take(l, b)

            next_own()
            for k in range(chips):
                pair(lax.rem(chip + k, chips))

        total = lows[...].astype(F32)
        for j in others:
            drain(lowr.at[j], lo_r.at[j])
        for j in others:
            total = total + lowr[j].astype(F32)
        lowt[...] = total.astype(BF16)
        sc[...] = dot(lowt[: 2 * rank], down, TN).reshape(seqs, seq, hw)
        for k in range(1, chips):
            j = flip(chip, k, chips)
            drain(xrecv.at[j], x_r.at[j])

        def gather_up(n, carry):
            xx, m = lax.div(n, micro), lax.rem(n, micro)
            value = sc[n] + cown[n]
            for k in range(1, chips):
                value = value + xrecv[flip(chip, k, chips), n].astype(F32)
            value = gains * value
            sc[n] = value
            rs_own[pl.ds(n, 1), :] = to_row(
                jnp.sum(act[l, xx, 3, m].astype(F32) * value, axis=-1, keepdims=True)
            )
            return carry

        lax.fori_loop(0, seqs, gather_up, 0)
        for k, j in enumerate(others):
            remote(rs_own, rsr.at[f], rs_s.at[k], rs_r.at[f], device(j)).start()
        for j in others:
            drain(rsr.at[j], rs_r.at[j])
        correction = rs_own[...]
        for j in others:
            correction = correction + rsr[j]
        crow[...] = correction * (1.0 / features)

        @pl.when(i > 0)
        def _():
            for xx in range(PAIR):
                drain(og.at[xx], o_s.at[xx])

        def settle(n, carry):
            xx, m = lax.div(n, micro), lax.rem(n, micro)
            inverse = to_column(st[xx * sections + l, pl.ds(m, 1), :])
            corrected = to_column(crow[pl.ds(n, 1), :])
            hidden = act[l, xx, 3, m].astype(F32)
            og[xx, m] = (
                og[xx, m].astype(F32) + inverse * sc[n] - hidden * (inverse * inverse * inverse * corrected)
            ).astype(BF16)
            return carry

        lax.fori_loop(0, seqs, settle, 0)
        for xx in range(PAIR):
            mine = (x == xx) & (s == l)

            @pl.when(mine)
            def _():
                pltpu.make_async_copy(og.at[xx], out_ig.at[0, :, 0, :, col_of(f)], o_s.at[xx]).start()

            @pl.when(jnp.logical_not(mine))
            def _():
                remote(
                    og.at[xx], out_ig.at[0, :, 0, :, col_of(f)], o_s.at[xx], o_r.at[f], (PAIR * a + xx, l)
                ).start()

        gr[l, a, : 2 * rank] = dot(lowt[: 2 * rank], normed, NN).astype(BF16)
        gr[l, a, 2 * rank : 3 * rank] = (
            adapter_scale * dot(lowt[2 * rank : 3 * rank], flat(ab[:, :, :hw]), NN)
        ).astype(BF16)
        gr[l, a, 3 * rank :] = (adapter_scale * dot(lowt[3 * rank :], flat(ab[:, :, 2 * hw :]), NN)).astype(BF16)
        for k in range(1, planes):
            remote(
                gr.at[l, a], gr.at[l, a], g_s.at[l, k], g_r.at[l, a], (PAIR * lax.rem(a + k, planes) + x, s)
            ).start()

        for k in range(cols - 1):
            drain(lows, lo_s.at[k])
            drain(rs_own, rs_s.at[k])
        for p in range(chips):
            drain(cs.at[p], d_s.at[p])
        for k in range(1, chips):
            j = flip(chip, k, chips)
            drain(xs.at[j], x_s.at[j])
        return carry

    lax.fori_loop(0, layers, layer, 0)
    finish_grads(0)

    for xx in range(PAIR):
        drain(og.at[xx], o_s.at[xx])
    for j in others:
        drain(out_ig.at[0, :, 0, :, col_of(j)], o_r.at[j])
        drain(out_g.at[:, col_of(j)], f_r.at[j])
    for k in range(1, sections):
        drain(ad.at[0], ad_s.at[k])
        drain(gn.at[0], gn_s.at[k])
    drain(og.at[0], cot_s.at[0])
    for k in range(cols - 1):
        drain(wbuf.at[0, 0, pl.ds(0, rows_w), :], w_s.at[k])
        drain(act.at[0, 0, pl.ds(0, 3)], q_s.at[k])
        drain(act.at[0, 0, 3], h_s.at[k])
        drain(st_own, st_s.at[k])

    def sent(l, carry):
        for i, d in enumerate((2, -2, 1, -1)):
            if abs(d) >= planes:
                continue

            @pl.when((a + d >= 0) & (a + d < planes))
            def _():
                drain(wbuf.at[l, a], z_s.at[l, i])

        for d in range(2, planes):
            for b in (a - d, a + d):

                @pl.when((b >= 0) & (b < planes))
                def _():
                    passed_on(l, b, lambda copy: copy.wait_send())

        for k in range(1, planes):
            drain(gr.at[l, a], g_s.at[l, k])
        for xx in range(PAIR):
            drain(gf.at[l], f_s.at[l, xx])
        return carry

    lax.fori_loop(0, layers, sent, 0)


def on_device(n_dp, layers, *args):
    hidden, cot, w, down = args[0], args[4], args[6], args[9]
    micro, seq, features = cot.shape[0], cot.shape[2], cot.shape[3]
    batch = cot.shape[1] * n_dp
    rank, rows_w = down.shape[1], w.shape[1]
    planes, cols = n_dp // PAIR, PAIR * layers
    chips, hw, seqs = cols // 2, features // cols, PAIR * micro
    rows = seqs * seq
    pad = -(-micro // 8) * 8
    pads = -(-seqs // 8) * 8
    dma = pltpu.SemaphoreType.DMA
    vm = pltpu.VMEM
    scratch = [
        vm((layers, planes, PAIR * rows_w, 3 * hw), BF16),
        vm((layers, PAIR, 4, micro, seq, hw), BF16),
        vm((micro, seq, features), BF16),
        vm((PAIR, micro, seq, hw), BF16),
        vm((seqs, seq, 3 * hw), BF16),
        vm((seqs, seq, hw), BF16),
        vm((layers, 4 * rank, hw), BF16),
        vm((layers, 1, hw), F32),
        vm((cols, pad, 128), F32),
        vm((pad, 128), F32),
        vm((4 * rank, rows), BF16),
        vm((cols, 4 * rank, rows), BF16),
        vm((4 * rank, rows), BF16),
        vm((chips, seqs, seq, hw), BF16),
        vm((chips, seqs, seq, hw), BF16),
        vm((seqs, seq, hw), F32),
        vm((seqs, seq, hw), F32),
        vm((chips, seqs, seq, hw), BF16),
        vm((chips, seqs, seq, hw), BF16),
        vm((seqs, seq, hw), F32),
        vm((pads, 128), F32),
        vm((cols, pads, 128), F32),
        vm((pads, 128), F32),
        vm((layers, planes, 4 * rank, hw), BF16),
        vm((layers, 4 * rank, hw), F32),
    ]
    semaphores = [
        dma((cols,)), dma((cols,)), dma((cols,)), dma((cols,)), dma((cols,)), dma((cols,)),
        dma((layers,)), dma((layers,)), dma((layers,)), dma((layers,)), dma((1,)), dma((2,)), dma,
        dma((cols,)), dma((cols,)),
        dma((layers, 4)), dma((layers, planes)), dma((layers, planes)),
        dma((cols,)), dma((cols,)), dma((chips,)), dma((chips,)), dma((chips,)), dma((chips,)),
        dma((cols,)), dma((cols,)), dma((PAIR,)), dma((cols,)),
        dma((layers, planes)), dma((layers, planes)), dma((layers, PAIR)), dma((cols,)),
    ]
    total_scale = (micro * batch * seq) ** (-0.5)
    any_space = pl.BlockSpec(memory_space=pl.ANY)
    input_grad, grads = pl.pallas_call(
        functools.partial(kernel, n_dp, layers, micro, seq, features, rank, rows_w, total_scale),
        out_shape=(
            jax.ShapeDtypeStruct(hidden.shape, BF16),
            jax.ShapeDtypeStruct((4 * rank, features), F32),
        ),
        in_specs=[any_space] * len(args),
        out_specs=(any_space, any_space),
        scratch_shapes=scratch + semaphores,
        compiler_params=pltpu.CompilerParams(
            collective_id=0, has_side_effects=True, vmem_limit_bytes=60 * 1024 * 1024
        ),
        name="section_backward",
    )(*args)
    return (
        input_grad,
        grads[None, :rank],
        grads[None, 2 * rank : 3 * rank],
        grads[None, rank : 2 * rank],
        grads[None, 3 * rank :],
    )


def solution(mesh):
    rows = P("section", None, "dp", None, None)
    cut = P("section", "dp", None)
    small = P("section", None, None)
    return jax.shard_map(
        functools.partial(on_device, mesh.shape["dp"], mesh.shape["section"]),
        mesh=mesh,
        in_specs=(rows,) * 4 + (P(None, "dp", None, None), P("section", None)) + (cut,) * 3 + (small,) * 4,
        out_specs=(rows,) + (small,) * 4,
        check_vma=False,
    )
```

profile of v0, /device:TPU:1, one launch (start us, length us, event | category | flops | bytes accessed | tf_op | source)
XLA Modules:
  0.0 348.2 jit_solution(10260085764703451597)
XLA Ops:
  0.6 342.9 %section_backward.1 = (bf16[1,4,1,96,2048]{4,3,2,1,0:T(8,128)(2,1)}, f32[64,2048]{1,0:T(8,128)}) custom-call(bf16[1,4,1,96,2048]{4,3,2,1,0:T(8,128)(2,1)} %hid.1, bf16[1,4,1,96,2048]{4,3,2,1,0:T(8,128)(2,1)} %que.1, bf16[1,4,1,96,2048]{4,3,2,1,0:T(8,128)(2,1)} %key.1, bf16[1,4,1,96,2048]{4,3,2,1,0:T(8,128)(2,1)} %val.1, bf16[4,1,96,2048]{3,2,1,0:T(8,128)(2,1)} %cot.1, ...), custom_call_target="tpu_custom_call" | custom-call | tf_op jit(solution)/shard_map/section_backward/pallas_call | solution.py:501
  343.6 1.9 slice_bitcast_fusion
  345.4 2.7 copy.19
where the time goes:
time: 355 us; the launch traced here: 348 us
  Pallas kernels  343 us (97%)
  local copies, waits for them, and re-layouts  4.62 us (1%)
    pallas_call x1, Pallas kernels, on_device(): pl.pallas_call(functools.partial(kernel, n_dp, layers, micro, seq, featur...  343 us

commit v1 on v0

v1 whole, which is shorter than its diff:
```python
import functools

import jax
import jax.numpy as jnp
from jax import lax
from jax.experimental import pallas as pl
from jax.experimental.pallas import tpu as pltpu
from jax.sharding import PartitionSpec as P

HEAD_DIM = 128
adapter_scale = 2.0
norm_eps = 1e-05
NN = (((1,), (0,)), ((), ()))
NT = (((1,), (1,)), ((), ()))
TN = (((0,), (0,)), ((), ()))
F32 = jnp.float32
BF16 = jnp.bfloat16
MESH = pl.DeviceIdType.MESH
PAIR = 2


def dot(a, b, dims):
    return lax.dot_general(a, b, dims, preferred_element_type=F32)


def drain(ref, sem):
    pltpu.make_async_copy(ref, ref, sem).wait()


def remote(src, dst, send, recv, device):
    return pltpu.make_async_remote_copy(
        src_ref=src, dst_ref=dst, send_sem=send, recv_sem=recv, device_id=device, device_id_type=MESH
    )


def flip(value, k, size):
    if size & (size - 1):
        return lax.rem(value + k, size)
    out, bit = 0, 1
    while bit < size:
        out = out + bit * lax.rem(lax.div(value, bit) + (k // bit) % 2, 2)
        bit *= 2
    return out


def kernel(
    n_dp, layers, micro, seq, features, rank, rows_w, total_scale,
    hid, que, key, val, cot, gain, wq, wk, wv, dq, uq, dv, uv,
    out_ig, out_g,
    wbuf, act, hown, og, ab, nrm, ad, gn, st, st_own, lows, lowr, norms, normr, lowt,
    cs, crecv, ctmp, xs, xrecv, sc, rs_own, rsr, crow, gr, gf,
    w_s, w_r, q_s, q_r, h_s, h_r, ad_s, ad_r, gn_s, gn_r, cot_s, cot_r, hown_sem, st_s, st_r,
    z_s, z_r, rel_s, lo_s, lo_r, ln_s, ln_r, d_s, d_r, x_s, x_r, rs_s, rs_r, o_s, o_r, g_s, g_r, f_s, f_r,
):
    sections = layers
    planes = n_dp // PAIR
    cols = PAIR * sections
    chips = cols // 2
    hw = features // cols
    heads = hw // HEAD_DIM
    seqs = PAIR * micro
    block = PAIR * rows_w
    groups = 2 * heads
    spread = chips * HEAD_DIM
    dp, s = lax.axis_index("dp"), lax.axis_index("section")
    a, x = lax.div(dp, PAIR), lax.rem(dp, PAIR)
    f = x * sections + s
    c = lax.rem(f, 2)
    chip = lax.div(f, 2)

    def device(j):
        return (PAIR * a + lax.div(j, sections), lax.rem(j, sections))

    others = [flip(f, k, cols) for k in range(1, cols)]

    def wide(j, ref):
        for u in range(heads):
            at = ((lax.rem(j, 2) * heads + u) * chips + lax.div(j, 2)) * HEAD_DIM
            yield ref.at[..., pl.ds(pl.multiple_of(at, HEAD_DIM), HEAD_DIM)], pl.ds(u * HEAD_DIM, HEAD_DIM)

    barrier = pltpu.get_barrier_semaphore()
    for j in others:
        pl.semaphore_signal(barrier, inc=1, device_id=device(j), device_id_type=MESH)
    for k in range(1, planes):
        pl.semaphore_signal(
            barrier, inc=1, device_id=(PAIR * lax.rem(a + k, planes) + x, s), device_id_type=MESH
        )
    pl.semaphore_wait(barrier, cols - 1 + planes - 1)

    own_hidden = pltpu.make_async_copy(hid.at[0, :, 0], hown, hown_sem)
    own_hidden.start()
    for k in range(sections):
        s2 = s if k == 0 else flip(s, k, sections)
        j = x * sections + s2
        for i, ref in enumerate((dq, dv, uq, uv)):
            for src, at in wide(j, ref.at[0]):
                dst = ad.at[s, pl.ds(i * rank, rank), at]
                if k == 0:
                    pltpu.make_async_copy(src, dst, ad_r.at[s]).start()
                else:
                    remote(src, dst, ad_s.at[k], ad_r.at[s], (dp, s2)).start()
        for src, at in wide(j, gain):
            dst = gn.at[s, :, at]
            if k == 0:
                pltpu.make_async_copy(src, dst, gn_r.at[s]).start()
            else:
                remote(src, dst, gn_s.at[k], gn_r.at[s], (dp, s2)).start()
    mirror = (PAIR * a + 1 - x, s)
    for src, at in wide((1 - x) * sections + s, cot.at[:, 0]):
        remote(src, og.at[x, :, :, at], cot_s.at[0], cot_r.at[0], mirror).start()
    for src, at in wide(f, cot.at[:, 0]):
        pltpu.make_async_copy(src, og.at[x, :, :, at], cot_r.at[1]).start()

    def weights(j):
        for i, ref in enumerate((wq, wk, wv)):
            for u, (src, at) in enumerate(wide(j, ref.at[0])):
                yield src, wbuf.at[s, a, pl.ds(x * rows_w, rows_w), pl.ds(i * hw + u * HEAD_DIM, HEAD_DIM)]

    def saved(j, which=(0, 1, 2)):
        for i in which:
            for src, at in wide(j, (que, key, val)[i].at[0, :, 0]):
                yield src, act.at[s, x, i, :, :, at]

    def inputs(j):
        for src, at in wide(j, hid.at[0, :, 0]):
            yield src, act.at[s, x, 3, :, :, at]

    for group, recv in ((weights, w_r), (saved, q_r), (inputs, h_r)):
        for src, dst in group(f):
            pltpu.make_async_copy(src, dst, recv.at[f]).start()

    def spread_out(group, send, recv):
        for k, j in enumerate(others):
            for src, dst in group(j):
                remote(src, dst, send.at[k], recv.at[f], device(j)).start()

    early = lax.rem(layers - 1 - s, 2) == 0
    spread_out(weights, w_s, w_r)

    @pl.when(early)
    def _():
        spread_out(saved, q_s, q_r)
        spread_out(inputs, h_s, h_r)

    def z_half(l, xx):
        part = wbuf.at[l, a, pl.ds(xx * rows_w, rows_w), :]
        drain(part, w_r.at[xx * sections + l])
        for i, d in enumerate((2, -2, 1, -1)):
            if abs(d) >= planes:
                continue

            @pl.when((a + d >= 0) & (a + d < planes))
            def _():
                remote(part, part, z_s.at[l, i], z_r.at[l, a], (PAIR * (a + d) + x, s)).start()

    z_half(s, x)

    def z_own(l):
        for xx in range(PAIR):

            @pl.when((l != s) | (xx != x))
            def _():
                z_half(l, xx)

    eye = lax.broadcasted_iota(jnp.int32, (seq, 128), 0) == lax.broadcasted_iota(jnp.int32, (seq, 128), 1)

    def to_row(column):
        return jnp.sum(jnp.where(eye, column, 0.0), axis=0, keepdims=True)

    def to_column(row):
        return jnp.sum(jnp.where(eye, row, 0.0), axis=1, keepdims=True)

    own_hidden.wait()

    def inverse_of(m, carry):
        floated = hown[m].astype(F32)
        inverse = lax.rsqrt(jnp.mean(floated * floated, axis=-1, keepdims=True) + norm_eps)
        st_own[pl.ds(m, 1), :] = to_row(inverse)
        return carry

    lax.fori_loop(0, micro, inverse_of, 0)
    st[f] = st_own[...]
    for k, j in enumerate(others):
        remote(st_own, st.at[f], st_s.at[k], st_r.at[f], device(j)).start()

    def passed_on(l, b, todo):
        for direction in (1, -1):

            @pl.when(((a - b) * direction >= 2) & (a + direction >= 0) & (a + direction < planes))
            def _():
                todo(
                    remote(
                        wbuf.at[l, b], wbuf.at[l, b], rel_s.at[l, b], z_r.at[l, b],
                        (PAIR * (a + direction) + x, s),
                    )
                )

    def take(l, b):
        drain(wbuf.at[l, b], z_r.at[l, b])
        passed_on(l, b, lambda copy: copy.start())

    scale = HEAD_DIM ** (-0.5)
    causal = lax.broadcasted_iota(jnp.int32, (seq, seq), 1) <= lax.broadcasted_iota(jnp.int32, (seq, seq), 0)
    z_own(layers - 1)

    def finish_grads(l):
        for k in range(1, planes):
            b = lax.rem(a + k, planes)
            drain(gr.at[l, b], g_r.at[l, b])
        total = gr[l, 0].astype(F32)
        for b in range(1, planes):
            total = total + gr[l, b].astype(F32)
        gf[l] = total * total_scale
        for xx in range(PAIR):
            mine = (x == xx) & (s == l)
            for dst, at in wide(f, out_g):

                @pl.when(mine)
                def _():
                    pltpu.make_async_copy(gf.at[l, :, at], dst, f_s.at[l, xx]).start()

                @pl.when(jnp.logical_not(mine))
                def _():
                    remote(gf.at[l, :, at], dst, f_s.at[l, xx], f_r.at[f], (PAIR * a + xx, l)).start()

    def layer(i, carry):
        l = layers - 1 - i
        for xx in range(PAIR):
            drain(act.at[l, xx, pl.ds(0, 3)], q_r.at[xx * sections + l])

        @pl.when(i == 0)
        def _():
            @pl.when(jnp.logical_not(early))
            def _():
                spread_out(lambda j: saved(j, (0, 1)), q_s, q_r)

            drain(og.at[0], cot_r.at[0])
            drain(og.at[0], cot_r.at[1])

        def next_own():
            @pl.when(l > 0)
            def _():
                z_own(l - 1)

        ordered = planes == 4 and groups == 4
        upper = lax.div(a, 2)
        near = a + upper * (3 - 2 * a)
        relays = (a == 1) | (a == 2)

        def nearest(k):
            lower = lax.rem(near + k, 2) if k < 2 else k
            return lower + upper * (3 - 2 * lower)

        if ordered:

            @pl.when(relays & (i > 0))
            def _():
                take(l, nearest(3))

            pl.when(i > 0)(next_own)

        def attention(n, carry):
            xx, m = lax.div(n, micro), lax.rem(n, micro)
            for h in range(heads):
                at = pl.ds(h * HEAD_DIM, HEAD_DIM)
                q, k, v = (act[l, xx, t, m, :, at] for t in range(3))
                g = og[xx, m, :, at]
                scores = jnp.where(causal, dot(q, k, NT) * scale, -1e30)
                grown = jnp.exp(scores - jnp.max(scores, axis=-1, keepdims=True))
                attend = grown / jnp.sum(grown, axis=-1, keepdims=True)
                attend_grad = dot(g, v, NT)
                value_grad = dot(attend.astype(BF16), g, TN)
                row_total = jnp.sum(attend * attend_grad, axis=-1, keepdims=True)
                score_grad = (attend * (attend_grad - row_total) * scale).astype(BF16)
                ab[n, :, at] = dot(score_grad, k, NN).astype(BF16)
                ab[n, :, pl.ds(hw + h * HEAD_DIM, HEAD_DIM)] = dot(score_grad, q, TN).astype(BF16)
                ab[n, :, pl.ds(2 * hw + h * HEAD_DIM, HEAD_DIM)] = value_grad.astype(BF16)
            return carry

        lax.fori_loop(0, seqs, attention, 0)

        def flat(value):
            return value.reshape(-1, value.shape[-1])

        if ordered:

            @pl.when(relays & (i == 0))
            def _():
                take(l, nearest(3))

            pl.when(i == 0)(next_own)

        drain(ad.at[l], ad_r.at[l])
        lows[:rank] = (adapter_scale * dot(ad[l, 2 * rank : 3 * rank], flat(ab[:, :, :hw]), NT)).astype(BF16)
        lows[rank:] = (adapter_scale * dot(ad[l, 3 * rank :], flat(ab[:, :, 2 * hw :]), NT)).astype(BF16)
        for k, j in enumerate(others):
            remote(lows, lowr.at[f], lo_s.at[k], lo_r.at[f], device(j)).start()
        down = ad[l, : 2 * rank]

        def normalise_all():
            for xx in range(PAIR):
                j = xx * sections + l
                drain(act.at[l, xx, 3], h_r.at[j])

                @pl.when(j != f)
                def _():
                    drain(st.at[j], st_r.at[j])

            drain(gn.at[l], gn_r.at[l])

            def normalise(n, carry):
                xx, m = lax.div(n, micro), lax.rem(n, micro)
                inverse = to_column(st[xx * sections + l, pl.ds(m, 1), :])
                nrm[n] = (act[l, xx, 3, m].astype(F32) * inverse * gn[l]).astype(BF16)
                return carry

            lax.fori_loop(0, seqs, normalise, 0)
            norms[...] = dot(down, flat(nrm[...]), NT).astype(BF16)
            for k, j in enumerate(others):
                remote(norms, normr.at[f], ln_s.at[k], ln_r.at[f], device(j)).start()

        partner = device(flip(f, 1, cols))

        def group(t):
            if spread == block:
                w = wbuf.at[l, t]
            else:
                w = wbuf.at[l, pl.ds(t * (spread // block), spread // block)]

            def half(xx):
                tokens = flat(ab[pl.ds(xx * micro, micro)])
                return dot(tokens, flat(w[...]), NT).reshape(micro, seq, spread)

            cs[t] = half(1 - c).astype(BF16)
            to_partner = remote(cs.at[t], crecv.at[t], d_s.at[t], d_r.at[t], partner)
            to_partner.start()
            ctmp[...] = half(c)
            to_partner.wait_recv()
            total = ctmp[...] + crecv[t].astype(F32)
            core, u = lax.div(t, heads), lax.rem(t, heads)
            for i in range(chips):
                piece = total[:, :, i * HEAD_DIM : (i + 1) * HEAD_DIM].astype(BF16)
                target = 2 * i + core

                @pl.when(target == f)
                def _():
                    xrecv[u, chip, c] = piece

                @pl.when(target != f)
                def _():
                    xs[t, i] = piece
                    remote(
                        xs.at[t, i], xrecv.at[u, chip, c], x_s.at[t, i], x_r.at[u, chip, c], device(target)
                    ).start()

        def summed(own, received, sems):
            for j in others:
                drain(received.at[j], sems.at[j])
            total = own[...].astype(F32)
            for j in others:
                total = total + received[j].astype(F32)
            return total.astype(BF16)

        def gradients():
            lowt[: 2 * rank] = summed(lows, lowr, lo_r)
            lowt[2 * rank :] = summed(norms, normr, ln_r)
            gr[l, a, : 2 * rank] = dot(lowt[: 2 * rank], flat(nrm[...]), NN).astype(BF16)
            gr[l, a, 2 * rank : 3 * rank] = (
                adapter_scale * dot(lowt[2 * rank : 3 * rank], flat(ab[:, :, :hw]), NN)
            ).astype(BF16)
            gr[l, a, 3 * rank :] = (
                adapter_scale * dot(lowt[3 * rank :], flat(ab[:, :, 2 * hw :]), NN)
            ).astype(BF16)
            for k in range(1, planes):
                there = (PAIR * lax.rem(a + k, planes) + x, s)
                remote(gr.at[l, a], gr.at[l, a], g_s.at[l, k], g_r.at[l, a], there).start()
            sc[...] = dot(lowt[: 2 * rank], down, TN).reshape(seqs, seq, hw)

        if ordered:
            pl.when(i > 0)(normalise_all)
            for k in range(4):
                t = nearest(k)
                if k == 1 or k == 2:
                    take(l, t)
                if k == 3:
                    pl.when(i == 0)(normalise_all)
                    gradients()

                    @pl.when(jnp.logical_not(relays))
                    def _():
                        take(l, t)

                group(t)
        else:
            for d in range(1, planes):
                for b in (a - d, a + d):

                    @pl.when((b >= 0) & (b < planes))
                    def _():
                        take(l, b)

            next_own()
            normalise_all()
            gradients()
            for t in range(groups):
                group(jnp.int32(t))
        pl.when(l == 0)(functools.partial(finish_grads, 0))

        for u in range(heads):
            for j in range(chips):
                for cc in range(2):

                    @pl.when((j != chip) | (cc != c))
                    def _():
                        drain(xrecv.at[u, j, cc], x_r.at[u, j, cc])

        def gather_up(n, carry):
            xx, m = lax.div(n, micro), lax.rem(n, micro)
            sums = []
            for u in range(heads):
                value = sc[n, :, u * HEAD_DIM : (u + 1) * HEAD_DIM]
                for j in range(chips):
                    value = value + xrecv[u, j, xx, m].astype(F32)
                value = gn[l, :, u * HEAD_DIM : (u + 1) * HEAD_DIM] * value
                sc[n, :, u * HEAD_DIM : (u + 1) * HEAD_DIM] = value
                sums.append(act[l, xx, 3, m, :, u * HEAD_DIM : (u + 1) * HEAD_DIM].astype(F32) * value)
            rs_own[pl.ds(n, 1), :] = to_row(jnp.sum(sum(sums), axis=-1, keepdims=True))
            return carry

        lax.fori_loop(0, seqs, gather_up, 0)
        for k, j in enumerate(others):
            remote(rs_own, rsr.at[f], rs_s.at[k], rs_r.at[f], device(j)).start()
        for j in others:
            drain(rsr.at[j], rs_r.at[j])
        correction = rs_own[...]
        for j in others:
            correction = correction + rsr[j]
        crow[...] = correction * (1.0 / features)

        @pl.when(i > 0)
        def _():
            for xx in range(PAIR):
                drain(og.at[xx], o_s.at[xx])

        def settle(n, carry):
            xx, m = lax.div(n, micro), lax.rem(n, micro)
            inverse = to_column(st[xx * sections + l, pl.ds(m, 1), :])
            corrected = to_column(crow[pl.ds(n, 1), :])
            hidden = act[l, xx, 3, m].astype(F32)
            og[xx, m] = (
                og[xx, m].astype(F32) + inverse * sc[n] - hidden * (inverse * inverse * inverse * corrected)
            ).astype(BF16)
            return carry

        lax.fori_loop(0, seqs, settle, 0)

        @pl.when(i == 0)
        def _():
            @pl.when(jnp.logical_not(early))
            def _():
                spread_out(lambda j: saved(j, (2,)), q_s, q_r)
                spread_out(inputs, h_s, h_r)

        for xx in range(PAIR):
            mine = (x == xx) & (s == l)
            for dst, at in wide(f, out_ig.at[0, :, 0]):
                src = og.at[xx, :, :, at]

                @pl.when(mine)
                def _():
                    pltpu.make_async_copy(src, dst, o_s.at[xx]).start()

                @pl.when(jnp.logical_not(mine))
                def _():
                    remote(src, dst, o_s.at[xx], o_r.at[f], (PAIR * a + xx, l)).start()

        @pl.when(i > 0)
        def _():
            finish_grads(l + 1)

        for k in range(cols - 1):
            drain(lows, lo_s.at[k])
            drain(norms, ln_s.at[k])
            drain(rs_own, rs_s.at[k])
        for t in range(groups):
            drain(cs.at[t], d_s.at[t])
            for j in range(chips):

                @pl.when(2 * j + t // heads != f)
                def _():
                    drain(xs.at[t, j], x_s.at[t, j])

        return carry

    lax.fori_loop(0, layers, layer, 0)

    for xx in range(PAIR):
        drain(og.at[xx], o_s.at[xx])
    for j in others:
        drain(og.at[0], o_r.at[j])
        drain(gf.at[0], f_r.at[j])
    for k in range(1, sections):
        drain(ad.at[0], ad_s.at[k])
        drain(gn.at[0], gn_s.at[k])
    drain(og.at[0], cot_s.at[0])
    for k in range(cols - 1):
        drain(wbuf.at[0, 0, pl.ds(0, rows_w), :], w_s.at[k])
        drain(act.at[0, 0, pl.ds(0, 3)], q_s.at[k])
        drain(act.at[0, 0, 3], h_s.at[k])
        drain(st_own, st_s.at[k])

    def sent(l, carry):
        for i, d in enumerate((2, -2, 1, -1)):
            if abs(d) >= planes:
                continue

            @pl.when((a + d >= 0) & (a + d < planes))
            def _():
                drain(wbuf.at[l, a], z_s.at[l, i])

        for d in range(2, planes):
            for b in (a - d, a + d):

                @pl.when((b >= 0) & (b < planes))
                def _():
                    passed_on(l, b, lambda copy: copy.wait_send())

        for k in range(1, planes):
            drain(gr.at[l, a], g_s.at[l, k])
        for xx in range(PAIR):
            drain(gf.at[l], f_s.at[l, xx])
        return carry

    lax.fori_loop(0, layers, sent, 0)


def on_device(n_dp, layers, *args):
    hidden, cot, w, down = args[0], args[4], args[6], args[9]
    micro, seq, features = cot.shape[0], cot.shape[2], cot.shape[3]
    batch = cot.shape[1] * n_dp
    rank, rows_w = down.shape[1], w.shape[1]
    planes, cols = n_dp // PAIR, PAIR * layers
    chips, hw, seqs = cols // 2, features // cols, PAIR * micro
    heads = hw // HEAD_DIM
    groups, spread = 2 * heads, chips * HEAD_DIM
    rows = seqs * seq
    pad = -(-micro // 8) * 8
    pads = -(-seqs // 8) * 8
    dma = pltpu.SemaphoreType.DMA
    vm = pltpu.VMEM
    scratch = [
        vm((layers, planes, PAIR * rows_w, 3 * hw), BF16),
        vm((layers, PAIR, 4, micro, seq, hw), BF16),
        vm((micro, seq, features), BF16),
        vm((PAIR, micro, seq, hw), BF16),
        vm((seqs, seq, 3 * hw), BF16),
        vm((seqs, seq, hw), BF16),
        vm((layers, 4 * rank, hw), BF16),
        vm((layers, 1, hw), F32),
        vm((cols, pad, 128), F32),
        vm((pad, 128), F32),
        vm((2 * rank, rows), BF16),
        vm((cols, 2 * rank, rows), BF16),
        vm((2 * rank, rows), BF16),
        vm((cols, 2 * rank, rows), BF16),
        vm((4 * rank, rows), BF16),
        vm((groups, micro, seq, spread), BF16),
        vm((groups, micro, seq, spread), BF16),
        vm((micro, seq, spread), F32),
        vm((groups, chips, micro, seq, HEAD_DIM), BF16),
        vm((heads, chips, 2, micro, seq, HEAD_DIM), BF16),
        vm((seqs, seq, hw), F32),
        vm((pads, 128), F32),
        vm((cols, pads, 128), F32),
        vm((pads, 128), F32),
        vm((layers, planes, 4 * rank, hw), BF16),
        vm((layers, 4 * rank, hw), F32),
    ]
    semaphores = [
        dma((cols,)), dma((cols,)), dma((cols,)), dma((cols,)), dma((cols,)), dma((cols,)),
        dma((layers,)), dma((layers,)), dma((layers,)), dma((layers,)), dma((1,)), dma((2,)), dma,
        dma((cols,)), dma((cols,)),
        dma((layers, 4)), dma((layers, planes)), dma((layers, planes)),
        dma((cols,)), dma((cols,)), dma((cols,)), dma((cols,)), dma((groups,)), dma((groups,)),
        dma((groups, chips)), dma((heads, chips, 2)),
        dma((cols,)), dma((cols,)), dma((PAIR,)), dma((cols,)),
        dma((layers, planes)), dma((layers, planes)), dma((layers, PAIR)), dma((cols,)),
    ]
    total_scale = (micro * batch * seq) ** (-0.5)
    any_space = pl.BlockSpec(memory_space=pl.ANY)
    input_grad, grads = pl.pallas_call(
        functools.partial(kernel, n_dp, layers, micro, seq, features, rank, rows_w, total_scale),
        out_shape=(
            jax.ShapeDtypeStruct(hidden.shape, BF16),
            jax.ShapeDtypeStruct((4 * rank, features), F32),
        ),
        in_specs=[any_space] * len(args),
        out_specs=(any_space, any_space),
        scratch_shapes=scratch + semaphores,
        compiler_params=pltpu.CompilerParams(
            collective_id=0, has_side_effects=True, vmem_limit_bytes=60 * 1024 * 1024
        ),
        name="section_backward",
    )(*args)
    return (
        input_grad,
        grads[None, :rank],
        grads[None, 2 * rank : 3 * rank],
        grads[None, rank : 2 * rank],
        grads[None, 3 * rank :],
    )


def solution(mesh):
    rows = P("section", None, "dp", None, None)
    cut = P("section", "dp", None)
    small = P("section", None, None)
    return jax.shard_map(
        functools.partial(on_device, mesh.shape["dp"], mesh.shape["section"]),
        mesh=mesh,
        in_specs=(rows,) * 4 + (P(None, "dp", None, None), P("section", None)) + (cut,) * 3 + (small,) * 4,
        out_specs=(rows,) + (small,) * 4,
        check_vma=False,
    )
```

time: 355 us -> 302 us (0.85); the launches traced: 348 us -> 302 us
  Pallas kernels: 343 us -> 297 us
    pallas_call x1, Pallas kernels: 343 us -> 297 us  [on_device(): pl.pallas_call(functools.partial(kernel, n_dp, layers, micro, seq, featur...]
where the time goes in v1:
time: 302 us
  Pallas kernels  297 us (98%)
  local copies, waits for them, and re-layouts  4.62 us (2%)
    pallas_call x1, Pallas kernels, on_device(): pl.pallas_call(functools.partial(kernel, n_dp, layers, micro, seq, featur...  297 us

profile of v1, /device:TPU:1, one launch (start us, length us, event | category | flops | bytes accessed | tf_op | source)
XLA Modules:
  0.0 302.2 jit_solution(1770535508208705127)
XLA Ops:
  0.6 296.9 %section_backward.1 = (bf16[1,4,1,96,2048]{4,3,2,1,0:T(8,128)(2,1)}, f32[64,2048]{1,0:T(8,128)}) custom-call(bf16[1,4,1,96,2048]{4,3,2,1,0:T(8,128)(2,1)} %hid.1, bf16[1,4,1,96,2048]{4,3,2,1,0:T(8,128)(2,1)} %que.1, bf16[1,4,1,96,2048]{4,3,2,1,0:T(8,128)(2,1)} %key.1, bf16[1,4,1,96,2048]{4,3,2,1,0:T(8,128)(2,1)} %val.1, bf16[4,1,96,2048]{3,2,1,0:T(8,128)(2,1)} %cot.1, ...), custom_call_target="tpu_custom_call" | custom-call | tf_op jit(solution)/shard_map/section_backward/pallas_call | solution.py:591
  297.5 1.9 slice_bitcast_fusion
  299.4 2.7 copy.19

commit v2 on v1

--- a/solution.py
+++ b/solution.py
@@ -47,10 +47,10 @@
     n_dp, layers, micro, seq, features, rank, rows_w, total_scale,
     hid, que, key, val, cot, gain, wq, wk, wv, dq, uq, dv, uv,
     out_ig, out_g,
-    wbuf, act, hown, og, ab, nrm, ad, gn, st, st_own, lows, lowr, norms, normr, lowt,
+    wbuf, act, hown, og, ab, nrm, ad, gn, st, st_own, both, pair_r, pair_t, chip_r, lowt,
     cs, crecv, ctmp, xs, xrecv, sc, rs_own, rsr, crow, gr, gf,
     w_s, w_r, q_s, q_r, h_s, h_r, ad_s, ad_r, gn_s, gn_r, cot_s, cot_r, hown_sem, st_s, st_r,
-    z_s, z_r, rel_s, lo_s, lo_r, ln_s, ln_r, d_s, d_r, x_s, x_r, rs_s, rs_r, o_s, o_r, g_s, g_r, f_s, f_r,
+    z_s, z_r, rel_s, lp_s, lp_r, lx_s, lx_r, lt_s, lt_r, d_s, d_r, x_s, x_r, rs_s, rs_r, o_s, o_r, g_s, g_r, f_s, f_r,
 ):
     sections = layers
     planes = n_dp // PAIR
@@ -135,10 +135,10 @@
                 remote(src, dst, send.at[k], recv.at[f], device(j)).start()
 
     early = lax.rem(layers - 1 - s, 2) == 0
-    spread_out(weights, w_s, w_r)
 
     @pl.when(early)
     def _():
+        spread_out(weights, w_s, w_r)
         spread_out(saved, q_s, q_r)
         spread_out(inputs, h_s, h_r)
 
@@ -225,23 +225,6 @@
 
     def layer(i, carry):
         l = layers - 1 - i
-        for xx in range(PAIR):
-            drain(act.at[l, xx, pl.ds(0, 3)], q_r.at[xx * sections + l])
-
-        @pl.when(i == 0)
-        def _():
-            @pl.when(jnp.logical_not(early))
-            def _():
-                spread_out(lambda j: saved(j, (0, 1)), q_s, q_r)
-
-            drain(og.at[0], cot_r.at[0])
-            drain(og.at[0], cot_r.at[1])
-
-        def next_own():
-            @pl.when(l > 0)
-            def _():
-                z_own(l - 1)
-
         ordered = planes == 4 and groups == 4
         upper = lax.div(a, 2)
         near = a + upper * (3 - 2 * a)
@@ -251,13 +234,30 @@
             lower = lax.rem(near + k, 2) if k < 2 else k
             return lower + upper * (3 - 2 * lower)
 
+        def pass_layer(m):
+            @pl.when(relays)
+            def _():
+                take(m, nearest(3))
+
+        def next_own(m):
+            @pl.when(m > 0)
+            def _():
+                z_own(m - 1)
+
         if ordered:
 
-            @pl.when(relays & (i > 0))
-            def _():
-                take(l, nearest(3))
-
-            pl.when(i > 0)(next_own)
+            @pl.when((i == 1) | (i > 2))
+            def _():
+                pass_layer(l)
+                next_own(l)
+
+        for xx in range(PAIR):
+            drain(act.at[l, xx, pl.ds(0, 3)], q_r.at[xx * sections + l])
+
+        @pl.when(i == 0)
+        def _():
+            drain(og.at[0], cot_r.at[0])
+            drain(og.at[0], cot_r.at[1])
 
         def attention(n, carry):
             xx, m = lax.div(n, micro), lax.rem(n, micro)
@@ -284,17 +284,19 @@
 
         if ordered:
 
-            @pl.when(relays & (i == 0))
-            def _():
-                take(l, nearest(3))
-
-            pl.when(i == 0)(next_own)
+            @pl.when(i == 0)
+            def _():
+                pass_layer(l)
 
         drain(ad.at[l], ad_r.at[l])
-        lows[:rank] = (adapter_scale * dot(ad[l, 2 * rank : 3 * rank], flat(ab[:, :, :hw]), NT)).astype(BF16)
-        lows[rank:] = (adapter_scale * dot(ad[l, 3 * rank :], flat(ab[:, :, 2 * hw :]), NT)).astype(BF16)
-        for k, j in enumerate(others):
-            remote(lows, lowr.at[f], lo_s.at[k], lo_r.at[f], device(j)).start()
+        both[0, :rank] = (adapter_scale * dot(ad[l, 2 * rank : 3 * rank], flat(ab[:, :, :hw]), NT)).astype(BF16)
+        both[0, rank:] = (adapter_scale * dot(ad[l, 3 * rank :], flat(ab[:, :, 2 * hw :]), NT)).astype(BF16)
+        partner = device(flip(f, 1, cols))
+
+        @pl.when(c == 1)
+        def _():
+            remote(both.at[0], pair_r, lp_s.at[0], lp_r.at[0], partner).start()
+
         down = ad[l, : 2 * rank]
 
         def normalise_all():
@@ -315,11 +317,27 @@
                 return carry
 
             lax.fori_loop(0, seqs, normalise, 0)
-            norms[...] = dot(down, flat(nrm[...]), NT).astype(BF16)
-            for k, j in enumerate(others):
-                remote(norms, normr.at[f], ln_s.at[k], ln_r.at[f], device(j)).start()
-
-        partner = device(flip(f, 1, cols))
+            both[1] = dot(down, flat(nrm[...]), NT).astype(BF16)
+
+            @pl.when(c == 0)
+            def _():
+                remote(both.at[1], pair_r, lp_s.at[0], lp_r.at[0], partner).start()
+
+        def over_pair():
+            drain(pair_r, lp_r.at[0])
+            pair_t[...] = (both[c].astype(F32) + pair_r[...].astype(F32)).astype(BF16)
+            for k in range(1, chips):
+                target = device(2 * flip(chip, k, chips) + c)
+                remote(pair_t, chip_r.at[chip], lx_s.at[k], lx_r.at[chip], target).start()
+
+        def over_chips():
+            total = pair_t[...].astype(F32)
+            for k in range(1, chips):
+                drain(chip_r.at[flip(chip, k, chips)], lx_r.at[flip(chip, k, chips)])
+            for k in range(1, chips):
+                total = total + chip_r[flip(chip, k, chips)].astype(F32)
+            lowt[c] = total.astype(BF16)
+            remote(lowt.at[c], lowt.at[c], lt_s.at[0], lt_r.at[0], partner).start()
 
         def group(t):
             if spread == block:
@@ -353,44 +371,42 @@
                         xs.at[t, i], xrecv.at[u, chip, c], x_s.at[t, i], x_r.at[u, chip, c], device(target)
                     ).start()
 
-        def summed(own, received, sems):
-            for j in others:
-                drain(received.at[j], sems.at[j])
-            total = own[...].astype(F32)
-            for j in others:
-                total = total + received[j].astype(F32)
-            return total.astype(BF16)
+        def send_late():
+            @pl.when(jnp.logical_not(early))
+            def _():
+                spread_out(weights, w_s, w_r)
+                spread_out(lambda j: saved(j, (0,)), q_s, q_r)
 
         def gradients():
-            lowt[: 2 * rank] = summed(lows, lowr, lo_r)
-            lowt[2 * rank :] = summed(norms, normr, ln_r)
-            gr[l, a, : 2 * rank] = dot(lowt[: 2 * rank], flat(nrm[...]), NN).astype(BF16)
-            gr[l, a, 2 * rank : 3 * rank] = (
-                adapter_scale * dot(lowt[2 * rank : 3 * rank], flat(ab[:, :, :hw]), NN)
-            ).astype(BF16)
-            gr[l, a, 3 * rank :] = (
-                adapter_scale * dot(lowt[3 * rank :], flat(ab[:, :, 2 * hw :]), NN)
-            ).astype(BF16)
+            drain(lowt.at[1 - c], lt_r.at[0])
+            gr[l, a, : 2 * rank] = dot(lowt[0], flat(nrm[...]), NN).astype(BF16)
+            gr[l, a, 2 * rank : 3 * rank] = (adapter_scale * dot(lowt[1, :rank], flat(ab[:, :, :hw]), NN)).astype(BF16)
+            gr[l, a, 3 * rank :] = (adapter_scale * dot(lowt[1, rank:], flat(ab[:, :, 2 * hw :]), NN)).astype(BF16)
             for k in range(1, planes):
                 there = (PAIR * lax.rem(a + k, planes) + x, s)
                 remote(gr.at[l, a], gr.at[l, a], g_s.at[l, k], g_r.at[l, a], there).start()
-            sc[...] = dot(lowt[: 2 * rank], down, TN).reshape(seqs, seq, hw)
+            sc[...] = dot(lowt[0], down, TN).reshape(seqs, seq, hw)
 
         if ordered:
-            pl.when(i > 0)(normalise_all)
+            pl.when(i > 1)(normalise_all)
             for k in range(4):
                 t = nearest(k)
                 if k == 1 or k == 2:
                     take(l, t)
                 if k == 3:
-                    pl.when(i == 0)(normalise_all)
-                    gradients()
+
+                    pl.when(i == 0)(functools.partial(next_own, l))
+                    pl.when(i < 2)(normalise_all)
+                    pl.when((i < 2) & (c == 1))(over_pair)
 
                     @pl.when(jnp.logical_not(relays))
                     def _():
                         take(l, t)
 
                 group(t)
+                if k == 0:
+                    pl.when((i > 1) | (c == 0))(over_pair)
+                    pl.when(i == 0)(send_late)
         else:
             for d in range(1, planes):
                 for b in (a - d, a + d):
@@ -399,11 +415,21 @@
                     def _():
                         take(l, b)
 
-            next_own()
+            pl.when(i == 0)(send_late)
+            next_own(l)
             normalise_all()
-            gradients()
+            over_pair()
             for t in range(groups):
                 group(jnp.int32(t))
+        over_chips()
+        gradients()
+        if ordered:
+
+            @pl.when((i == 1) & (l > 0))
+            def _():
+                pass_layer(l - 1)
+                next_own(l - 1)
+
         pl.when(l == 0)(functools.partial(finish_grads, 0))
 
         for u in range(heads):
@@ -458,7 +484,7 @@
         def _():
             @pl.when(jnp.logical_not(early))
             def _():
-                spread_out(lambda j: saved(j, (2,)), q_s, q_r)
+                spread_out(lambda j: saved(j, (1, 2)), q_s, q_r)
                 spread_out(inputs, h_s, h_r)
 
         for xx in range(PAIR):
@@ -479,9 +505,11 @@
             finish_grads(l + 1)
 
         for k in range(cols - 1):
-            drain(lows, lo_s.at[k])
-            drain(norms, ln_s.at[k])
             drain(rs_own, rs_s.at[k])
+        drain(both.at[0], lp_s.at[0])
+        drain(lowt.at[0], lt_s.at[0])
+        for k in range(1, chips):
+            drain(pair_t, lx_s.at[k])
         for t in range(groups):
             drain(cs.at[t], d_s.at[t])
             for j in range(chips):
@@ -559,11 +587,11 @@
         vm((layers, 1, hw), F32),
         vm((cols, pad, 128), F32),
         vm((pad, 128), F32),
+        vm((2, 2 * rank, rows), BF16),
         vm((2 * rank, rows), BF16),
-        vm((cols, 2 * rank, rows), BF16),
         vm((2 * rank, rows), BF16),
-        vm((cols, 2 * rank, rows), BF16),
-        vm((4 * rank, rows), BF16),
+        vm((chips, 2 * rank, rows), BF16),
+        vm((2, 2 * rank, rows), BF16),
         vm((groups, micro, seq, spread), BF16),
         vm((groups, micro, seq, spread), BF16),
         vm((micro, seq, spread), F32),
@@ -581,7 +609,7 @@
         dma((layers,)), dma((layers,)), dma((layers,)), dma((layers,)), dma((1,)), dma((2,)), dma,
         dma((cols,)), dma((cols,)),
         dma((layers, 4)), dma((layers, planes)), dma((layers, planes)),
-        dma((cols,)), dma((cols,)), dma((cols,)), dma((cols,)), dma((groups,)), dma((groups,)),
+        dma((1,)), dma((1,)), dma((chips,)), dma((chips,)), dma((1,)), dma((1,)), dma((groups,)), dma((groups,)),
         dma((groups, chips)), dma((heads, chips, 2)),
         dma((cols,)), dma((cols,)), dma((PAIR,)), dma((cols,)),
         dma((layers, planes)), dma((layers, planes)), dma((layers, PAIR)), dma((cols,)),

time: 302 us -> 277 us (0.917); the launches traced: 302 us -> 274 us
  Pallas kernels: 297 us -> 269 us
    pallas_call x1, Pallas kernels: 297 us -> 269 us  [on_device(): pl.pallas_call(functools.partial(kernel, n_dp, layers, micro, seq, featur...]
where the time goes in v2:
time: 277 us; the launch traced here: 274 us
  Pallas kernels  269 us (97%)
  local copies, waits for them, and re-layouts  4.62 us (2%)
    pallas_call x1, Pallas kernels, on_device(): pl.pallas_call(functools.partial(kernel, n_dp, layers, micro, seq, featur...  269 us

profile of v2, /device:TPU:1, one launch (start us, length us, event | category | flops | bytes accessed | tf_op | source)
XLA Modules:
  0.0 273.9 jit_solution(14365464896092420055)
XLA Ops:
  0.6 268.7 %section_backward.1 = (bf16[1,4,1,96,2048]{4,3,2,1,0:T(8,128)(2,1)}, f32[64,2048]{1,0:T(8,128)}) custom-call(bf16[1,4,1,96,2048]{4,3,2,1,0:T(8,128)(2,1)} %hid.1, bf16[1,4,1,96,2048]{4,3,2,1,0:T(8,128)(2,1)} %que.1, bf16[1,4,1,96,2048]{4,3,2,1,0:T(8,128)(2,1)} %key.1, bf16[1,4,1,96,2048]{4,3,2,1,0:T(8,128)(2,1)} %val.1, bf16[4,1,96,2048]{3,2,1,0:T(8,128)(2,1)} %cot.1, ...), custom_call_target="tpu_custom_call" | custom-call | tf_op jit(solution)/shard_map/section_backward/pallas_call | solution.py:619
  269.3 1.9 slice_bitcast_fusion
  271.2 2.7 copy.19

commit v3 on v2

--- a/solution.py
+++ b/solution.py
@@ -277,7 +277,7 @@
                 ab[n, :, pl.ds(2 * hw + h * HEAD_DIM, HEAD_DIM)] = value_grad.astype(BF16)
             return carry
 
-        lax.fori_loop(0, seqs, attention, 0)
+        lax.fori_loop(0, seqs, attention, 0, unroll=2)
 
         def flat(value):
             return value.reshape(-1, value.shape[-1])
@@ -316,7 +316,7 @@
                 nrm[n] = (act[l, xx, 3, m].astype(F32) * inverse * gn[l]).astype(BF16)
                 return carry
 
-            lax.fori_loop(0, seqs, normalise, 0)
+            lax.fori_loop(0, seqs, normalise, 0, unroll=2)
             both[1] = dot(down, flat(nrm[...]), NT).astype(BF16)
 
             @pl.when(c == 0)
@@ -375,7 +375,6 @@
             @pl.when(jnp.logical_not(early))
             def _():
                 spread_out(weights, w_s, w_r)
-                spread_out(lambda j: saved(j, (0,)), q_s, q_r)
 
         def gradients():
             drain(lowt.at[1 - c], lt_r.at[0])
@@ -453,9 +452,17 @@
             rs_own[pl.ds(n, 1), :] = to_row(jnp.sum(sum(sums), axis=-1, keepdims=True))
             return carry
 
-        lax.fori_loop(0, seqs, gather_up, 0)
+        lax.fori_loop(0, seqs, gather_up, 0, unroll=2)
         for k, j in enumerate(others):
             remote(rs_own, rsr.at[f], rs_s.at[k], rs_r.at[f], device(j)).start()
+
+        @pl.when(i == 0)
+        def _():
+            @pl.when(jnp.logical_not(early))
+            def _():
+                spread_out(lambda j: saved(j, (0, 1, 2)), q_s, q_r)
+                spread_out(inputs, h_s, h_r)
+
         for j in others:
             drain(rsr.at[j], rs_r.at[j])
         correction = rs_own[...]
@@ -478,14 +485,7 @@
             ).astype(BF16)
             return carry
 
-        lax.fori_loop(0, seqs, settle, 0)
-
-        @pl.when(i == 0)
-        def _():
-            @pl.when(jnp.logical_not(early))
-            def _():
-                spread_out(lambda j: saved(j, (1, 2)), q_s, q_r)
-                spread_out(inputs, h_s, h_r)
+        lax.fori_loop(0, seqs, settle, 0, unroll=2)
 
         for xx in range(PAIR):
             mine = (x == xx) & (s == l)

time: 277 us -> 275 us (level)
  no operation moved by 1% of the time
where the time goes in v3:
time: 275 us; the launch traced here: 274 us
  Pallas kernels  269 us (98%)
  local copies, waits for them, and re-layouts  4.62 us (2%)
    pallas_call x1, Pallas kernels, on_device(): pl.pallas_call(functools.partial(kernel, n_dp, layers, micro, seq, featur...  269 us

profile of v3, /device:TPU:1, one launch (start us, length us, event | category | flops | bytes accessed | tf_op | source)
XLA Modules:
  0.0 274.2 jit_solution(18075996321446485686)
XLA Ops:
  0.6 268.9 %section_backward.1 = (bf16[1,4,1,96,2048]{4,3,2,1,0:T(8,128)(2,1)}, f32[64,2048]{1,0:T(8,128)}) custom-call(bf16[1,4,1,96,2048]{4,3,2,1,0:T(8,128)(2,1)} %hid.1, bf16[1,4,1,96,2048]{4,3,2,1,0:T(8,128)(2,1)} %que.1, bf16[1,4,1,96,2048]{4,3,2,1,0:T(8,128)(2,1)} %key.1, bf16[1,4,1,96,2048]{4,3,2,1,0:T(8,128)(2,1)} %val.1, bf16[4,1,96,2048]{3,2,1,0:T(8,128)(2,1)} %cot.1, ...), custom_call_target="tpu_custom_call" | custom-call | tf_op jit(solution)/shard_map/section_backward/pallas_call | solution.py:619
  269.5 1.9 slice_bitcast_fusion
  271.4 2.7 copy.19

commit v4 on v3

--- a/solution.py
+++ b/solution.py
@@ -316,7 +316,7 @@
                 nrm[n] = (act[l, xx, 3, m].astype(F32) * inverse * gn[l]).astype(BF16)
                 return carry
 
-            lax.fori_loop(0, seqs, normalise, 0, unroll=2)
+            lax.fori_loop(0, seqs, normalise, 0, unroll=4)
             both[1] = dot(down, flat(nrm[...]), NT).astype(BF16)
 
             @pl.when(c == 0)
@@ -452,7 +452,7 @@
             rs_own[pl.ds(n, 1), :] = to_row(jnp.sum(sum(sums), axis=-1, keepdims=True))
             return carry
 
-        lax.fori_loop(0, seqs, gather_up, 0, unroll=2)
+        lax.fori_loop(0, seqs, gather_up, 0, unroll=4)
         for k, j in enumerate(others):
             remote(rs_own, rsr.at[f], rs_s.at[k], rs_r.at[f], device(j)).start()
 
@@ -485,7 +485,7 @@
             ).astype(BF16)
             return carry
 
-        lax.fori_loop(0, seqs, settle, 0, unroll=2)
+        lax.fori_loop(0, seqs, settle, 0, unroll=4)
 
         for xx in range(PAIR):
             mine = (x == xx) & (s == l)

time: 275 us -> 275 us (level)
  no operation moved by 1% of the time
where the time goes in v4:
time: 275 us; the launch traced here: 274 us
  Pallas kernels  269 us (98%)
  local copies, waits for them, and re-layouts  4.62 us (2%)
    pallas_call x1, Pallas kernels, on_device(): pl.pallas_call(functools.partial(kernel, n_dp, layers, micro, seq, featur...  269 us

profile of v4, /device:TPU:1, one launch (start us, length us, event | category | flops | bytes accessed | tf_op | source)
XLA Modules:
  0.0 274.3 jit_solution(3065291854718678608)
XLA Ops:
  0.6 269.1 %section_backward.1 = (bf16[1,4,1,96,2048]{4,3,2,1,0:T(8,128)(2,1)}, f32[64,2048]{1,0:T(8,128)}) custom-call(bf16[1,4,1,96,2048]{4,3,2,1,0:T(8,128)(2,1)} %hid.1, bf16[1,4,1,96,2048]{4,3,2,1,0:T(8,128)(2,1)} %que.1, bf16[1,4,1,96,2048]{4,3,2,1,0:T(8,128)(2,1)} %key.1, bf16[1,4,1,96,2048]{4,3,2,1,0:T(8,128)(2,1)} %val.1, bf16[4,1,96,2048]{3,2,1,0:T(8,128)(2,1)} %cot.1, ...), custom_call_target="tpu_custom_call" | custom-call | tf_op jit(solution)/shard_map/section_backward/pallas_call | solution.py:619
  269.7 1.9 slice_bitcast_fusion
  271.6 2.7 copy.19
